TPU v7x, 32 devices: a whole 2x2x4 slice. The times are simulated.
32 devices in a mesh: row: 8 (over y, x, core), col: 4 (over z).
Axes of the slice: x: 2, y: 2, z: 4, core: 2. Of those that a mesh axis runs over, the one named last changes fastest.
Arguments:
- source: float32 [512, 512, 512], P('row', 'col'), may hold values from -8 to 8
- basis_x: float32 [512, 512], replicated, may hold values from -0.25 to 0.25
- basis_y: float32 [512, 512], replicated, may hold values from -0.25 to 0.25
- basis_z: float32 [512, 512], replicated, may hold values from -0.25 to 0.25
- eigen_x: float32 [512], replicated, may hold values from 0.1 to 10
- eigen_y: float32 [512], replicated, may hold values from 0.1 to 10
- eigen_z: float32 [512], replicated, may hold values from 0.1 to 10
Outputs:
- solution: float32 [512, 512, 512], P('row', 'col')
All inputs are finite; a program needn't handle non-finite values.
Results may differ from a plain program's by a relative error of at most 0.00007.
Values sent between devices are 32-bit elements; how exact they have to be, the bound alone decides.
No kernel may reach another device: no remote copies, remote signals or barrier semaphores. Data moves between devices by JAX's collectives and lax.ppermute only.
A program may use at most 128 MiB of HBM per device.

v0:
```python
import jax
import jax.numpy as jnp
from jax import lax
from jax.sharding import PartitionSpec as P

HIGH = lax.Precision.HIGHEST


def divide(field, first, second, third):
    denom = first[:, None, None] + second[None, :, None] + third[None, None, :]
    return field / denom


def piece_of(values, index, count):
    return lax.dynamic_slice_in_dim(values, index * count, count, 0)


def local(source, basis_x, basis_y, basis_z, eigen_x, eigen_y, eigen_z):
    row_index = lax.axis_index("row")
    col_index = lax.axis_index("col")
    rows_n = lax.axis_size("row")
    cols_n = lax.axis_size("col")
    nx_full = basis_x.shape[0]
    ny_full = basis_y.shape[0]
    field = jnp.einsum("ck,abc->abk", basis_z, source, precision=HIGH)
    field = field[None]
    field = lax.all_to_all(field, ("row", "col"), split_axis=3, concat_axis=0, tiled=True)
    planes = field.shape[3]
    field = field.reshape(rows_n, cols_n, field.shape[1], field.shape[2], planes)
    blocks_x = basis_x.reshape(rows_n, nx_full // rows_n, nx_full)
    blocks_y = basis_y.reshape(cols_n, ny_full // cols_n, ny_full)
    field = jnp.einsum("rai,rcabk->icbk", blocks_x, field, precision=HIGH)
    field = jnp.einsum("cbj,icbk->ijk", blocks_y, field, precision=HIGH)
    part_z = piece_of(eigen_z, row_index * cols_n + col_index, planes)
    field = divide(field, eigen_x, eigen_y, part_z)
    field = jnp.einsum("cbj,ijk->icbk", blocks_y, field, precision=HIGH)
    field = jnp.einsum("rai,icbk->rcabk", blocks_x, field, precision=HIGH)
    field = field.reshape(rows_n * cols_n, field.shape[2], field.shape[3], planes)
    field = lax.all_to_all(field, ("row", "col"), split_axis=0, concat_axis=3, tiled=True)
    field = jnp.einsum("ck,abk->abc", basis_z, field[0], precision=HIGH)
    return field


def solution(mesh):
    placed = (P("row", "col", None), P(), P(), P(), P(), P(), P())
    return jax.shard_map(
        local, mesh=mesh, in_specs=placed, out_specs=P("row", "col", None), check_vma=False
    )
```

profile of v0, /device:TPU:1, one launch (start us, length us, event | category | flops | bytes accessed | tf_op | source)
XLA Modules:
  0.0 1082.5 jit_solution(10844230199941101817)
XLA Ops:
  0.0 0.0 copy-start
  0.0 32.2 %convolution_bitcast_fusion.1 = f32[1,64,128,512]{3,2,1,0:T(8,128)} fusion(f32[64,128,512]{2,1,0:T(8,128)} %param.7, f32[512,512]{1,0:T(8,128)} %param.10), kind=kOutput, calls=%fused_computation.8 | convolution fusion | flops 25769803776 | bytes 34603008 | tf_op jit(solution)/shard_map/ck,abc->abk/dot_general | solution.py:25
  32.2 16.5 %copy.19 = f32[1,64,128,512]{2,1,0,3:T(8,128)} copy(f32[1,64,128,512]{3,2,1,0:T(8,128)} %convolution_bitcast_fusion.1) | data formatting | bytes 33554432 | tf_op jit(solution)/shard_map/broadcast_in_dim | solution.py:26
  48.7 0.0 copy-start.3
  48.7 0.0 copy-start.4
  48.7 7.5 all-to-all-start
  56.2 0.8 dynamic_slice.3
  57.0 0.0 copy-done.3
  57.0 0.0 copy-done.4
  57.0 0.1 broadcast_add_fusion
  57.1 355.5 %all-to-all-done = f32[1,64,128,512]{2,1,0,3:T(8,128)} async-done(((f32[1,64,128,512]{2,1,0,3:T(8,128)}), f32[1,64,128,512]{2,1,0,3:T(8,128)}, u32[]{:S(2)}, u32[]{:S(2)}) %all-to-all-start) | async-done | bytes 16777248 | tf_op jit(solution)/shard_map/all_to_all | solution.py:27
  412.6 30.6 %copy.22 = f32[8,4,64,128,16]{2,4,0,3,1:T(8,128)} copy(f32[8,4,64,128,16]{3,2,4,1,0:T(8,128)} %bitcast.29) | data formatting | bytes 33554432 | tf_op jit(solution)/shard_map/reshape | solution.py:29
  443.2 0.0 copy-done.2
  443.2 50.3 %convolution_bitcast_fusion = f32[512,4,128,16]{0,3,2,1:T(8,128)} fusion(f32[8,4,64,128,16]{2,4,0,3,1:T(8,128)} %copy.22, f32[8,64,512,1,1]{2,1,0,4,3:T(8,128)S(1)} %bitcast.65), kind=kOutput, calls=%fused_computation.7 | convolution fusion | flops 25769803776 | bytes 34603008 | tf_op jit(solution)/shard_map/rai,rcabk->icbk/dot_general | solution.py:32
  493.5 20.7 %copy.23 = f32[512,4,128,16]{2,3,1,0:T(8,128)} copy(f32[512,4,128,16]{0,3,2,1:T(8,128)} %convolution_bitcast_fusion) | data formatting | bytes 33554432 | tf_op jit(solution)/shard_map/rai,rcabk->icbk/dot_general | solution.py:32
  514.2 0.0 copy-done
  514.2 31.9 %bitcast_divide_fusion = f32[512,512,16]{1,2,0:T(8,128)} fusion(f32[512,4,128,16]{2,3,1,0:T(8,128)} %copy.23, f32[4,128,512,1]{2,1,0,3:T(8,128)S(1)} %bitcast.61, f32[16]{0:T(128)S(1)} %dynamic_slice.3, f32[512,512]{1,0:T(8,128)S(1)} %broadcast_add_fusion), kind=kOutput, calls=%fused_computation.2 | convolution fusion | flops 25778192384 | bytes 35651648 | tf_op jit(solution)/shard_map/cbj,icbk->ijk/dot_general | solution.py:33
  546.1 41.4 %fusion.2 = f32[512,16,4,128]{3,0,1,2:T(8,128)S(1)} fusion(f32[4,128,512,1]{2,1,3,0:T(8,128)S(1)} %bitcast.60, f32[512,512,16]{1,2,0:T(8,128)} %bitcast_divide_fusion), kind=kOutput, calls=%fused_computation.3 | convolution fusion | flops 25769803776 | bytes 34603008 | tf_op jit(solution)/shard_map/cbj,ijk->icbk/dot_general | solution.py:36
  587.5 30.2 %fusion.5 = f32[8,4,64,128,16]{3,2,0,4,1:T(8,128)} fusion(f32[8,64,512,1,1]{2,1,0,4,3:T(8,128)S(1)} %bitcast.66, f32[512,16,4,128]{3,0,1,2:T(8,128)S(1)} %fusion.2), kind=kOutput, calls=%fused_computation.6 | convolution fusion | flops 25769803776 | bytes 34603008 | tf_op jit(solution)/shard_map/rai,icbk->rcabk/dot_general | solution.py:37
  617.7 16.9 %copy.25 = f32[8,4,64,128,16]{3,4,2,1,0:T(8,128)S(1)} copy(f32[8,4,64,128,16]{3,2,0,4,1:T(8,128)} %fusion.5) | data formatting | bytes 33554432 | tf_op jit(solution)/shard_map/rai,icbk->rcabk/transpose | solution.py:37
  634.6 382.2 %all_to_all.30 = f32[32,64,128,16]{2,3,1,0:T(8,128)} all-to-all(f32[32,64,128,16]{2,3,1,0:T(8,128)S(1)} %bitcast.63), channel_id=1, replica_groups=mesh['row'=8,'col'=4] {'row','col'}, dimensions={0} | all-to-all | bytes 33554432 | tf_op jit(solution)/shard_map/all_to_all | solution.py:39
  1016.8 6.9 copy.26
  1023.7 0.0 copy-done.1
  1023.7 58.6 %fusion.8 = f32[64,128,512]{2,1,0:T(8,128)} fusion(f32[64,128,512]{1,2,0:T(8,128)S(1)} %bitcast.62, f32[512,512]{1,0:T(8,128)S(1)} %copy-done.1), kind=kOutput, calls=%fused_computation.9 | convolution fusion | flops 25769803776 | bytes 34603008 | tf_op jit(solution)/shard_map/ck,abk->abc/dot_general | solution.py:40
  (2 shorter events, 0.0 us)
Async XLA Ops:
  0.0 514.2 %copy-start = (f32[512,512]{1,0:T(8,128)S(1)}, f32[512,512]{1,0:T(8,128)}, u32[]{:S(2)}) copy-start(f32[512,512]{1,0:T(8,128)} %param.9) | copy-start | bytes 3145732
  48.7 8.3 copy-start.3
  48.7 8.3 copy-start.4
  48.7 363.9 %all-to-all-start = ((f32[1,64,128,512]{2,1,0,3:T(8,128)}), f32[1,64,128,512]{2,1,0,3:T(8,128)}, u32[]{:S(2)}, u32[]{:S(2)}) async-start(f32[1,64,128,512]{2,1,0,3:T(8,128)} %copy.19), calls=%async_computation | async-start | bytes 33554432 | tf_op jit(solution)/shard_map/all_to_all | solution.py:27
  412.6 30.6 %copy-start.2 = (f32[512,512]{1,0:T(8,128)S(1)}, f32[512,512]{1,0:T(8,128)}, u32[]{:S(2)}) copy-start(f32[512,512]{1,0:T(8,128)} %param.8) | copy-start | bytes 3145732
  1016.8 6.9 copy-start.1
where the time goes:
time: 1090 us; the launch traced here: 1080 us
  blocking collectives  382 us (35%)
  waiting for transfers between devices  356 us (33%)
  matrix products  245 us (22%)
  local copies, waits for them, and re-layouts  92.4 us (8%)
    all_to_all x1, blocking collectives, local(): lax.all_to_all(field, ('row', 'col'), split_axis=0, concat_axis=3, tiled=...  382 us
    all_to_all x1, waiting for transfers between devices, local(): lax.all_to_all(field, ('row', 'col'), split_axis=3, concat_axis=0, tiled=...  356 us
    dot_general x1, matrix products, local(): field = jnp.einsum('ck,abk->abc', basis_z, field[0], precision=HIGH)  58.6 us
    dot_general x1, matrix products, local(): field = jnp.einsum('rai,rcabk->icbk', blocks_x, field, precision=HIGH)  50.3 us
    dot_general x1, matrix products, local(): field = jnp.einsum('cbj,ijk->icbk', blocks_y, field, precision=HIGH)  41.4 us
    dot_general x1, matrix products, local(): field = jnp.einsum('ck,abc->abk', basis_z, source, precision=HIGH)  32.2 us
    dot_general x1, matrix products, local(): field = jnp.einsum('cbj,icbk->ijk', blocks_y, field, precision=HIGH)  31.9 us
    reshape x1, local copies, waits for them, and re-layouts, local(): field.reshape(rows_n, cols_n, field.shape[1], field.shape[2], planes)  30.6 us
  transfers between devices with their start and end apart: 1, of which 1 were waited for; matrix products, arithmetic and copies ran while one was open for 0% of the time, Pallas kernels for 0%

commit v1 on v0

v1 whole, which is shorter than its diff:
```python
import jax
import jax.numpy as jnp
from jax import lax
from jax.experimental import pallas as pl
from jax.experimental.pallas import tpu as pltpu
from jax.sharding import PartitionSpec as P


F32, BF16 = jnp.float32, jnp.bfloat16
CHUNKS = 4
PARTS = 4
LINES = 8
ROWS = 512


def halves(values):
    high = values.astype(BF16)
    return high, (values - high.astype(F32)).astype(BF16)


def product(left, right, dims=((1,), (0,))):
    def one(first, second):
        return lax.dot_general(first, second, (dims, ((), ())), preferred_element_type=F32)

    return one(left[0], right[0]) + (one(left[0], right[1]) + one(left[1], right[0]))


def cost(flops, values):
    return pl.CostEstimate(flops=3 * flops, bytes_accessed=4 * values, transcendentals=0)


def smem():
    return pl.BlockSpec(memory_space=pltpu.SMEM)


def whole(shape):
    return pl.BlockSpec(shape, lambda i: (0,) * len(shape))


def forward_z(basis, source, me, count, planes, chunks, at_line, lines):
    _, width, depth = source.shape
    full = basis.shape[1]
    step = min(LINES, lines)
    own = full // count
    starts = [(shift, chunk * planes) for chunk in chunks for shift in range(count)]
    total = len(starts) * planes

    def kernel(me_ref, basis_ref, source_ref, *refs):
        outs, (turned, high, low) = refs[:-3], refs[-3:]

        @pl.when(pl.program_id(0) == 0)
        def _():
            turned[...] = basis_ref[...].T
            for at, (shift, first) in enumerate(starts):
                block = lax.rem(me_ref[0] + shift, count) * own + first
                block = turned[pl.ds(pl.multiple_of(block, 8), planes), :]
                here = slice(at * planes, (at + 1) * planes)
                high[here], low[here] = halves(block)

        def pair(turn, carry):
            at = turn * 2
            block = source_ref[pl.ds(at, 2)].reshape(2 * width, depth)
            result = product((high[...], low[...]), halves(block), ((1,), (1,)))
            for place, out in enumerate(outs):
                flat = out.reshape(planes * step, width)
                rows = result[place * planes : (place + 1) * planes]
                flat[pl.ds(at, planes, stride=step), :] = rows[:, :width]
                flat[pl.ds(at + 1, planes, stride=step), :] = rows[:, width:]
            return carry

        lax.fori_loop(0, step // 2, pair, 0, unroll=2)

    return pl.pallas_call(
        kernel,
        grid=(lines // step,),
        in_specs=[
            smem(),
            whole((depth, full)),
            pl.BlockSpec((step, width, depth), lambda i: (i + at_line // step, 0, 0)),
        ],
        out_specs=[pl.BlockSpec((planes, step, width), lambda i: (0, i, 0))] * len(starts),
        out_shape=[jax.ShapeDtypeStruct((planes, lines, width), F32)] * len(starts),
        scratch_shapes=[pltpu.VMEM((full, depth), F32)] + [pltpu.VMEM((total, depth), BF16)] * 2,
        cost_estimate=cost(2 * total * lines * width * depth, lines * width * (depth + total)),
        name="forward_z",
    )(me, basis, source)


def prepare_z(basis, me, count):
    depth, full = basis.shape
    own = full // count

    def kernel(me_ref, basis_ref, high, low, turned):
        turned[...] = basis_ref[...].T
        parts = []
        for shift in range(count):
            block = lax.rem(me_ref[0] + (count - shift), count) * own
            parts.append(turned[pl.ds(pl.multiple_of(block, 8), own), :])
        high[...], low[...] = halves(jnp.concatenate(parts, axis=0).T)

    return pl.pallas_call(
        kernel,
        in_specs=[smem(), pl.BlockSpec(memory_space=pltpu.VMEM)],
        out_specs=[pl.BlockSpec(memory_space=pltpu.VMEM)] * 2,
        out_shape=[jax.ShapeDtypeStruct((depth, full), BF16)] * 2,
        scratch_shapes=[pltpu.VMEM((full, depth), F32)],
        cost_estimate=cost(depth * full, 2 * depth * full),
        name="prepare_z",
    )(me, basis)


def backward_z(basis, fields, last, count, total, at_line, result):
    depth, full = basis[0].shape
    planes, lines, width = last[0].shape
    step = min(LINES, lines)
    offset = at_line // step
    earlier = len(fields) // count
    held = [] if result is None else [result]

    def kernel(high, low, *refs):
        out = refs[-1]
        fields, last = refs[: count * earlier], refs[count * earlier : count * (earlier + 1)]

        def pair(turn, carry):
            at = turn * 2
            columns = []
            for line in (at, at + 1):
                parts = []
                for shift in range(count):
                    for ref in (*fields[shift * earlier : (shift + 1) * earlier], last[shift]):
                        parts.append(ref.reshape(planes * step, width)[pl.ds(line, planes, stride=step), :])
                columns.append(jnp.concatenate(parts, axis=0))
            result = product((high[...], low[...]), halves(jnp.concatenate(columns, axis=1)))
            out[at] = result[:, :width].T
            out[at + 1] = result[:, width:].T
            return carry

        lax.fori_loop(0, step // 2, pair, 0, unroll=2)

    return pl.pallas_call(
        kernel,
        grid=(lines // step,),
        in_specs=[whole((depth, full))] * 2
        + [pl.BlockSpec((planes, step, width), lambda i: (0, i + offset, 0))] * len(fields)
        + [pl.BlockSpec((planes, step, width), lambda i: (0, i, 0))] * count
        + [pl.BlockSpec(memory_space=pl.ANY)] * len(held),
        out_specs=pl.BlockSpec((step, width, depth), lambda i: (i + offset, 0, 0)),
        out_shape=jax.ShapeDtypeStruct((total, width, depth), F32),
        input_output_aliases={2 + len(fields) + count: 0} if held else {},
        cost_estimate=cost(2 * lines * width * depth * full, lines * width * (depth + full)),
        name="backward_z",
    )(*basis, *fields, *last, *held)


def y_grid(planes, lines):
    step = min(planes, max(1, ROWS // lines))
    return step, (planes // step,)


def forward_y(basis, fields, me):
    count, pieces = len(fields), len(fields[0])
    planes, piece, width = fields[0][0].shape
    lines = piece * pieces
    full = basis.shape[1]
    step, grid = y_grid(planes, lines)

    def kernel(me_ref, basis_ref, *refs):
        fields, out, high, low = refs[:-3], *refs[-3:]

        @pl.when(pl.program_id(0) == 0)
        def _():
            for shift in range(count):
                block = lax.rem(me_ref[0] + (count - shift), count) * width
                block = basis_ref[pl.ds(pl.multiple_of(block, 8), width), :]
                high[shift * width : (shift + 1) * width], low[shift * width : (shift + 1) * width] = halves(block)

        columns = []
        for shift in range(count):
            parts = [ref[...] for ref in fields[shift * pieces : (shift + 1) * pieces]]
            columns.append(jnp.concatenate(parts, axis=1).reshape(step * lines, width))
        field = jnp.concatenate(columns, axis=1)
        out[...] = product(halves(field), (high[...], low[...])).reshape(step, lines, full)

    return pl.pallas_call(
        kernel,
        grid=grid,
        in_specs=[smem(), whole(basis.shape)]
        + [pl.BlockSpec((step, piece, width), lambda i: (i, 0, 0))] * (count * pieces),
        out_specs=pl.BlockSpec((step, lines, full), lambda i: (i, 0, 0)),
        out_shape=jax.ShapeDtypeStruct((planes, lines, full), F32),
        scratch_shapes=[pltpu.VMEM((count * width, full), BF16)] * 2,
        cost_estimate=cost(2 * planes * lines * width * count * full, planes * lines * (width * count + full)),
        name="forward_y",
    )(me, basis, *[part for parts in fields for part in parts])


def backward_y(basis, field, me, count, pieces):
    planes, lines, full = field.shape
    width = basis.shape[0] // count
    piece = lines // pieces
    step, grid = y_grid(planes, lines)

    def kernel(me_ref, basis_ref, field_ref, *refs):
        outs, (high, low) = refs[:-2], refs[-2:]

        @pl.when(pl.program_id(0) == 0)
        def _():
            for shift in range(count):
                block = lax.rem(me_ref[0] + shift, count) * width
                block = basis_ref[pl.ds(pl.multiple_of(block, 8), width), :]
                high[shift * width : (shift + 1) * width], low[shift * width : (shift + 1) * width] = halves(block)

        field = field_ref[...].reshape(step * lines, full)
        result = product(halves(field), (high[...], low[...]), ((1,), (1,)))
        for shift in range(count):
            block = result[:, shift * width : (shift + 1) * width].reshape(step, lines, width)
            for at in range(pieces):
                outs[at * count + shift][...] = block[:, at * piece : (at + 1) * piece]

    return pl.pallas_call(
        kernel,
        grid=grid,
        in_specs=[smem(), whole(basis.shape), pl.BlockSpec((step, lines, full), lambda i: (i, 0, 0))],
        out_specs=[pl.BlockSpec((step, piece, width), lambda i: (i, 0, 0))] * (count * pieces),
        out_shape=[jax.ShapeDtypeStruct((planes, piece, width), F32)] * (count * pieces),
        scratch_shapes=[pltpu.VMEM((count * width, full), BF16)] * 2,
        cost_estimate=cost(2 * planes * lines * width * count * full, planes * lines * (width * count + full)),
        name="backward_y",
    )(me, basis, field)


def solve_x(field, basis, eigen_x, eigen_y, eigen_z):
    rows, planes, lines, full = field.shape
    nx = basis.shape[0]
    block = pl.BlockSpec((rows, 1, lines, full), lambda p: (0, p, 0, 0))

    def kernel(eig_ref, basis_ref, ex_ref, ey_ref, in_ref, out_ref, plain, turned):
        plane = pl.program_id(0)

        @pl.when(plane == 0)
        def _():
            plain[0], plain[1] = halves(basis_ref[...])
            turned[0], turned[1] = halves(basis_ref[...].T)

        field = in_ref[:, 0].reshape(rows * lines, full)
        field = product((turned[0], turned[1]), halves(field))
        field = field / (ex_ref[...] + ey_ref[...] + eig_ref[plane])
        field = product((plain[0], plain[1]), halves(field))
        out_ref[:, 0] = field.reshape(rows, lines, full)

    return pl.pallas_call(
        kernel,
        grid=(planes,),
        in_specs=[smem(), whole((nx, nx)), whole((nx, 1)), whole((1, full)), block],
        out_specs=block,
        out_shape=jax.ShapeDtypeStruct(field.shape, F32),
        scratch_shapes=[pltpu.VMEM((2, nx, nx), BF16)] * 2,
        cost_estimate=cost(4 * planes * nx * nx * full, 2 * planes * nx * full),
        name="solve_x",
    )(eigen_z, basis, eigen_x[:, None], eigen_y[None, :], field)


def local(source, basis_x, basis_y, basis_z, eigen_x, eigen_y, eigen_z):
    rows, cols = lax.axis_size("row"), lax.axis_size("col")
    row, col = lax.axis_index("row"), lax.axis_index("col")
    lines, _, _ = source.shape
    full = basis_z.shape[1]
    chunks = min(CHUNKS, full // (rows * cols))
    own = full // cols
    planes = own // chunks
    part = planes // rows
    me = jnp.reshape(col, (1,)).astype(jnp.int32)

    def along_col(fields):
        moved = [fields[0]]
        for shift in range(1, cols):
            ring = [(at, (at + shift) % cols) for at in range(cols)]
            moved.append(lax.ppermute(fields[shift], "col", ring))
        return moved

    def along_row(field):
        return lax.all_to_all(field, "row", split_axis=0, concat_axis=0, tiled=True)

    pieces = max(1, min(PARTS, lines // LINES))
    piece = lines // pieces
    first = []
    for at in range(pieces):
        sent = forward_z(basis_z, source, me, cols, planes, [0], at * piece, piece)
        first.append(along_col(sent))
    got = [[[part[shift] for part in first] for shift in range(cols)]]
    if chunks > 1:
        sent = forward_z(basis_z, source, me, cols, planes, range(1, chunks), 0, lines)
        for chunk in range(1, chunks):
            moved = along_col(sent[(chunk - 1) * cols : chunk * cols])
            got.append([[field] for field in moved])
    back = []
    for chunk in range(chunks):
        field = forward_y(basis_y, got[chunk], me)
        field = along_row(field.reshape(rows, part, lines, field.shape[2]))
        eigen = lax.dynamic_slice_in_dim(eigen_z, col * own + chunk * planes + row * part, part, 0)
        field = solve_x(field, basis_x, eigen_x, eigen_y, eigen)
        field = along_row(field)
        field = field.reshape(planes, lines, field.shape[3])
        final = chunk == chunks - 1
        sent = backward_y(basis_y, field, me, cols, pieces if final else 1)
        if not final:
            back.append(along_col(sent))
    fields = [moved[shift] for shift in range(cols) for moved in back]
    result = None
    ready = prepare_z(basis_z, me, cols)
    last = [along_col(sent[at * cols : (at + 1) * cols]) for at in range(pieces)]
    for at in range(pieces):
        result = backward_z(ready, fields, last[at], cols, lines, at * piece, result)
    return result


def solution(mesh):
    placed = (P("row", "col", None), P(), P(), P(), P(), P(), P())
    return jax.shard_map(
        local, mesh=mesh, in_specs=placed, out_specs=P("row", "col", None), check_vma=False
    )
```

time: 1090 us -> 1050 us (0.963)
  blocking collectives: 382 us -> 0 us
  starting transfers between devices: 7.5 us -> 345 us
  matrix products: 245 us -> 0 us
  Pallas kernels: 0 us -> 183 us
  waiting for transfers between devices: 356 us -> 514 us
  local copies, waits for them, and re-layouts: 92.4 us -> 9.14 us
    all_to_all x1 -> x0, blocking collectives: 382 us -> none  [local(): lax.all_to_all(field, ('row', 'col'), split_axis=0, concat_axis=3, tiled=...]
    ppermute x0 -> x42, waiting for transfers between devices: none -> 376 us  [along_col(): moved.append(lax.ppermute(fields[shift], 'col', ring))]
    ppermute x0 -> x42, starting transfers between devices: none -> 291 us  [along_col(): moved.append(lax.ppermute(fields[shift], 'col', ring))]
    dot_general x6 -> x0, matrix products: 245 us -> none  [the longest x1 58.6 us: local(): field = jnp.einsum('ck,abk->abc', basis_z, field[0], precision=HIGH)]
    all_to_all x1 -> x8, waiting for transfers between devices: 356 us -> 137 us  [along_row(): return lax.all_to_all(field, 'row', split_axis=0, concat_axis=0, tiled=True)]
    pallas_call x0 -> x22, Pallas kernels: none -> 183 us  [the longest x4 43.2 us: solve_x(): pl.pallas_call(kernel, grid=(planes,), in_specs=[smem(), whole((nx, nx)),...]
    all_to_all x1 -> x8, starting transfers between devices: 7.5 us -> 53.2 us  [along_row(): return lax.all_to_all(field, 'row', split_axis=0, concat_axis=0, tiled=True)]
    reshape x1 -> x0, local copies, waits for them, and re-layouts: 30.6 us -> none  [local(): field.reshape(rows_n, cols_n, field.shape[1], field.shape[2], planes)]
  transfers between devices with their start and end apart: 1 -> 50, of which waited for: 1 -> 22; matrix products, arithmetic and copies ran while one was open for 0% -> 0% of each run, Pallas kernels for 0% -> 15%
where the time goes in v1:
time: 1050 us
  waiting for transfers between devices  514 us (49%)
  starting transfers between devices  345 us (33%)
  Pallas kernels  183 us (17%)
    ppermute x42, waiting for transfers between devices, along_col(): moved.append(lax.ppermute(fields[shift], 'col', ring))  376 us
    ppermute x42, starting transfers between devices, along_col(): moved.append(lax.ppermute(fields[shift], 'col', ring))  291 us
    all_to_all x8, waiting for transfers between devices, along_row(): return lax.all_to_all(field, 'row', split_axis=0, concat_axis=0, tiled=True)  137 us
    all_to_all x8, starting transfers between devices, along_row(): return lax.all_to_all(field, 'row', split_axis=0, concat_axis=0, tiled=True)  53.2 us
    pallas_call x4, Pallas kernels, solve_x(): pl.pallas_call(kernel, grid=(planes,), in_specs=[smem(), whole((nx, nx)),...  43.2 us
    pallas_call x5, Pallas kernels, forward_z(): pl.pallas_call(kernel, grid=(lines // step,), in_specs=[smem(), whole((de...  42 us
    pallas_call x4, Pallas kernels, backward_z(): pl.pallas_call(kernel, grid=(lines // step,), in_specs=[whole((depth, ful...  34.7 us
    pallas_call x4, Pallas kernels, backward_y(): pl.pallas_call(kernel, grid=grid, in_specs=[smem(), whole(basis.shape), p...  30 us
  transfers between devices with their start and end apart: 50, of which 22 were waited for; matrix products, arithmetic and copies ran while one was open for 0% of the time, Pallas kernels for 15%

profile of v1, /device:TPU:1, one launch (start us, length us, event | category | flops | bytes accessed | tf_op | source)
XLA Modules:
  0.0 1050.3 jit_solution(14102114895418460132)
XLA Ops:
  109.0 18.9 %forward_z.9 = (f32[32,64,128]{2,1,0:T(8,128)}, f32[32,64,128]{2,1,0:T(8,128)}, f32[32,64,128]{2,1,0:T(8,128)}, f32[32,64,128]{2,1,0:T(8,128)}, f32[32,64,128]{2...) custom-call(s32[1]{0:T(128)} %bitcast.me_ref, ...), custom_call_target="tpu_custom_call" | custom-call | flops 9663676416 | bytes 29360128 | tf_op jit(solution)/shard_map/forward_z/pallas_call | solution.py:73
  135.8 22.6 %collective-permute-done.12.refs_1_ = f32[32,64,128]{2,1,0:T(8,128)S(1)} collective-permute-done((f32[32,64,128]{2,1,0:T(8,128)}, f32[32,64,128]{2,1,0:T(8,128)S(1)}, u32[]{:S(2)}, u32[]{:S(2)}) %collective-permute-start.12) | collective-permute-done | bytes 1048608 | tf_op jit(solution)/shard_map/ppermute | solution.py:278
  158.4 45.1 %collective-permute-done.13.refs_2_ = f32[32,64,128]{2,1,0:T(8,128)S(1)} collective-permute-done((f32[32,64,128]{2,1,0:T(8,128)}, f32[32,64,128]{2,1,0:T(8,128)S(1)}, u32[]{:S(2)}, u32[]{:S(2)}) %collective-permute-start.13) | collective-permute-done | bytes 1048608 | tf_op jit(solution)/shard_map/ppermute | solution.py:278
  217.6 22.3 %collective-permute-start.15 = (f32[32,64,128]{2,1,0:T(8,128)S(1)}, f32[32,64,128]{2,1,0:T(8,128)S(1)}, u32[]{:S(2)}, u32[]{:S(2)}) collective-permute-start(f32[32,64,128]{2,1,0:T(8,128)S(1)} %copy-done.18), channel_id=1, source_target_pairs={{0,1},{1,2},{2,3},{3,0},{4,5},{5,6},{6,7},{7,4},{8,9},{9,10},{10,1... | collective-permute-start | bytes 3145736 | tf_op jit(solution)/shard_map/ppermute | solution.py:278
  242.1 22.3 %collective-permute-done.15.refs_1_ = f32[32,64,128]{2,1,0:T(8,128)S(1)} collective-permute-done((f32[32,64,128]{2,1,0:T(8,128)S(1)}, f32[32,64,128]{2,1,0:T(8,128)S(1)}, u32[]{:S(2)}, u32[]{:S(2)}) %collective-permute-start.15) | collective-permute-done | bytes 1048608 | tf_op jit(solution)/shard_map/ppermute | solution.py:278
  264.4 45.2 %collective-permute-done.16.refs_2_ = f32[32,64,128]{2,1,0:T(8,128)S(1)} collective-permute-done((f32[32,64,128]{2,1,0:T(8,128)S(1)}, f32[32,64,128]{2,1,0:T(8,128)S(1)}, u32[]{:S(2)}, u32[]{:S(2)}) %collective-permute-start.16) | collective-permute-done | bytes 1048608 | tf_op jit(solution)/shard_map/ppermute | solution.py:278
  324.3 21.7 %collective-permute-start.27 = (f32[32,64,128]{2,1,0:T(8,128)S(1)}, f32[32,64,128]{2,1,0:T(8,128)S(1)}, u32[]{:S(2)}, u32[]{:S(2)}) collective-permute-start(f32[32,64,128]{2,1,0:T(8,128)S(1)} %copy-done.15), channel_id=1, source_target_pairs={{0,1},{1,2},{2,3},{3,0},{4,5},{5,6},{6,7},{7,4},{8,9},{9,10},{10,1... | collective-permute-start | bytes 3145736 | tf_op jit(solution)/shard_map/ppermute | solution.py:278
  348.1 23.0 %collective-permute-done.27.refs_1_ = f32[32,64,128]{2,1,0:T(8,128)S(1)} collective-permute-done((f32[32,64,128]{2,1,0:T(8,128)S(1)}, f32[32,64,128]{2,1,0:T(8,128)S(1)}, u32[]{:S(2)}, u32[]{:S(2)}) %collective-permute-start.27) | collective-permute-done | bytes 1048608 | tf_op jit(solution)/shard_map/ppermute | solution.py:278
  371.1 45.2 %collective-permute-done.28.refs_2_ = f32[32,64,128]{2,1,0:T(8,128)S(1)} collective-permute-done((f32[32,64,128]{2,1,0:T(8,128)S(1)}, f32[32,64,128]{2,1,0:T(8,128)S(1)}, u32[]{:S(2)}, u32[]{:S(2)}) %collective-permute-start.28) | collective-permute-done | bytes 1048608 | tf_op jit(solution)/shard_map/ppermute | solution.py:278
  443.2 33.1 %all-to-all-done.6.in_ref = f32[8,4,64,512]{3,2,1,0:T(8,128)} async-done(((f32[8,4,64,512]{3,2,1,0:T(8,128)}), f32[8,4,64,512]{3,2,1,0:T(8,128)}, u32[]{:S(2)}, u32[]{:S(2)}) %all-to-all-start.6) | async-done | bytes 4194336 | tf_op jit(solution)/shard_map/all_to_all | solution.py:282
  495.4 34.8 %all-to-all-done.1 = f32[8,4,64,512]{3,2,1,0:T(8,128)} async-done(((f32[8,4,64,512]{3,2,1,0:T(8,128)}), f32[8,4,64,512]{3,2,1,0:T(8,128)}, u32[]{:S(2)}, u32[]{:S(2)}) %all-to-all-start.1) | async-done | bytes 4194336 | tf_op jit(solution)/shard_map/all_to_all | solution.py:282
  549.1 34.8 %all-to-all-done.3 = f32[8,4,64,512]{3,2,1,0:T(8,128)} async-done(((f32[8,4,64,512]{3,2,1,0:T(8,128)}), f32[8,4,64,512]{3,2,1,0:T(8,128)}, u32[]{:S(2)}, u32[]{:S(2)}) %all-to-all-start.3) | async-done | bytes 4194336 | tf_op jit(solution)/shard_map/all_to_all | solution.py:282
  602.7 34.8 %all-to-all-done.7 = f32[8,4,64,512]{3,2,1,0:T(8,128)} async-done(((f32[8,4,64,512]{3,2,1,0:T(8,128)}), f32[8,4,64,512]{3,2,1,0:T(8,128)}, u32[]{:S(2)}, u32[]{:S(2)}) %all-to-all-start.7) | async-done | bytes 4194336 | tf_op jit(solution)/shard_map/all_to_all | solution.py:282
  653.1 21.7 %collective-permute-start.18 = (f32[32,64,128]{2,1,0:T(8,128)}, f32[32,64,128]{2,1,0:T(8,128)S(1)}, u32[]{:S(2)}, u32[]{:S(2)}) collective-permute-start(f32[32,64,128]{2,1,0:T(8,128)} %get-tuple-element.92), channel_id=1, source_target_pairs={{0,1},{1,2},{2,3},{3,0},{4,5},{5,6},{6,7},{7,4},{8,9},{9,10},{10,1... | collective-permute-start | bytes 3145736 | tf_op jit(solution)/shard_map/ppermute | solution.py:278
  699.7 45.1 %collective-permute-done.21.refs_6_ = f32[32,64,128]{2,1,0:T(8,128)S(1)} collective-permute-done((f32[32,64,128]{2,1,0:T(8,128)}, f32[32,64,128]{2,1,0:T(8,128)S(1)}, u32[]{:S(2)}, u32[]{:S(2)}) %collective-permute-start.21) | collective-permute-done | bytes 1048608 | tf_op jit(solution)/shard_map/ppermute | solution.py:278
  744.8 23.1 %collective-permute-start.41 = (f32[32,16,128]{2,1,0:T(8,128)}, f32[32,16,128]{2,1,0:T(8,128)}, u32[]{:S(2)}, u32[]{:S(2)}) collective-permute-start(f32[32,16,128]{2,1,0:T(8,128)} %get-tuple-element.120), channel_id=1, source_target_pairs={{0,3},{1,0},{2,1},{3,2},{4,7},{5,4},{6,5},{7,6},{8,11},{9,8},{10,9... | collective-permute-start | bytes 786440 | tf_op jit(solution)/shard_map/ppermute | solution.py:278
  775.5 24.7 %collective-permute-start.22 = (f32[32,64,128]{2,1,0:T(8,128)}, f32[32,64,128]{2,1,0:T(8,128)S(1)}, u32[]{:S(2)}, u32[]{:S(2)}) collective-permute-start(f32[32,64,128]{2,1,0:T(8,128)} %get-tuple-element.96), channel_id=1, source_target_pairs={{0,2},{1,3},{2,0},{3,1},{4,6},{5,7},{6,4},{7,5},{8,10},{9,11},{10,... | collective-permute-start | bytes 3145736 | tf_op jit(solution)/shard_map/ppermute | solution.py:278
  803.2 25.8 %collective-permute-done.40.refs_14_ = f32[32,16,128]{2,1,0:T(8,128)} collective-permute-done((f32[32,16,128]{2,1,0:T(8,128)}, f32[32,16,128]{2,1,0:T(8,128)}, u32[]{:S(2)}, u32[]{:S(2)}) %collective-permute-start.40) | collective-permute-done | bytes 262176 | tf_op jit(solution)/shard_map/ppermute | solution.py:278
  829.0 26.1 %collective-permute-start.20 = (f32[32,64,128]{2,1,0:T(8,128)}, f32[32,64,128]{2,1,0:T(8,128)}, u32[]{:S(2)}, u32[]{:S(2)}) collective-permute-start(f32[32,64,128]{2,1,0:T(8,128)} %get-tuple-element.94), channel_id=1, source_target_pairs={{0,1},{1,2},{2,3},{3,0},{4,5},{5,6},{6,7},{7,4},{8,9},{9,10},{10,1... | collective-permute-start | bytes 3145736 | tf_op jit(solution)/shard_map/ppermute | solution.py:278
  861.1 16.5 %collective-permute-start.30 = (f32[32,16,128]{2,1,0:T(8,128)}, f32[32,16,128]{2,1,0:T(8,128)S(1)}, u32[]{:S(2)}, u32[]{:S(2)}) collective-permute-start(f32[32,16,128]{2,1,0:T(8,128)} %get-tuple-element.106), channel_id=1, source_target_pairs={{0,1},{1,2},{2,3},{3,0},{4,5},{5,6},{6,7},{7,4},{8,9},{9,10},{10,1... | collective-permute-start | bytes 786440 | tf_op jit(solution)/shard_map/ppermute | solution.py:278
  877.7 24.3 %collective-permute-done.25.refs_10_ = f32[32,64,128]{2,1,0:T(8,128)S(1)} collective-permute-done((f32[32,64,128]{2,1,0:T(8,128)}, f32[32,64,128]{2,1,0:T(8,128)S(1)}, u32[]{:S(2)}, u32[]{:S(2)}) %collective-permute-start.25) | collective-permute-done | bytes 1048608 | tf_op jit(solution)/shard_map/ppermute | solution.py:278
  901.9 21.9 %collective-permute-start.31 = (f32[32,16,128]{2,1,0:T(8,128)}, f32[32,16,128]{2,1,0:T(8,128)}, u32[]{:S(2)}, u32[]{:S(2)}) collective-permute-start(f32[32,16,128]{2,1,0:T(8,128)} %get-tuple-element.107), channel_id=1, source_target_pairs={{0,2},{1,3},{2,0},{3,1},{4,6},{5,7},{6,4},{7,5},{8,10},{9,11},{10,... | collective-permute-start | bytes 786440 | tf_op jit(solution)/shard_map/ppermute | solution.py:278
  923.8 26.9 %collective-permute-start.36 = (f32[32,16,128]{2,1,0:T(8,128)}, f32[32,16,128]{2,1,0:T(8,128)}, u32[]{:S(2)}, u32[]{:S(2)}) collective-permute-start(f32[32,16,128]{2,1,0:T(8,128)} %get-tuple-element.114), channel_id=1, source_target_pairs={{0,1},{1,2},{2,3},{3,0},{4,5},{5,6},{6,7},{7,4},{8,9},{9,10},{10,1... | collective-permute-start | bytes 786440 | tf_op jit(solution)/shard_map/ppermute | solution.py:278
  963.9 17.8 %collective-permute-start.38 = (f32[32,16,128]{2,1,0:T(8,128)}, f32[32,16,128]{2,1,0:T(8,128)}, u32[]{:S(2)}, u32[]{:S(2)}) collective-permute-start(f32[32,16,128]{2,1,0:T(8,128)} %get-tuple-element.116), channel_id=1, source_target_pairs={{0,3},{1,0},{2,1},{3,2},{4,7},{5,4},{6,5},{7,6},{8,11},{9,8},{10,9... | collective-permute-start | bytes 786440 | tf_op jit(solution)/shard_map/ppermute | solution.py:278
  (188 shorter events, 372.1 us)
Async XLA Ops:
  103.9 108.4 %all-to-all-start = ((f32[8,4,64,512]{3,2,1,0:T(8,128)}), f32[8,4,64,512]{3,2,1,0:T(8,128)}, u32[]{:S(2)}, u32[]{:S(2)}) async-start(f32[8,4,64,512]{3,2,1,0:T(8,128)} %bitcast.12), calls=%async_computation | async-start | bytes 8388608 | tf_op jit(solution)/shard_map/all_to_all | solution.py:282
  133.6 69.9 %collective-permute-start.13 = (f32[32,64,128]{2,1,0:T(8,128)}, f32[32,64,128]{2,1,0:T(8,128)S(1)}, u32[]{:S(2)}, u32[]{:S(2)}) collective-permute-start(f32[32,64,128]{2,1,0:T(8,128)} %get-tuple-element.84), channel_id=1, source_target_pairs={{0,2},{1,3},{2,0},{3,1},{4,6},{5,7},{6,4},{7,5},{8,10},{9,11},{10,... | collective-permute-start | bytes 3145736 | tf_op jit(solution)/shard_map/ppermute | solution.py:278
  135.0 68.5 %collective-permute-start.14 = (f32[32,64,128]{2,1,0:T(8,128)}, f32[32,64,128]{2,1,0:T(8,128)S(1)}, u32[]{:S(2)}, u32[]{:S(2)}) collective-permute-start(f32[32,64,128]{2,1,0:T(8,128)} %get-tuple-element.85), channel_id=1, source_target_pairs={{0,3},{1,0},{2,1},{3,2},{4,7},{5,4},{6,5},{7,6},{8,11},{9,8},{10,9... | collective-permute-start | bytes 3145736 | tf_op jit(solution)/shard_map/ppermute | solution.py:278
  212.3 106.6 %all-to-all-start.2 = ((f32[8,4,64,512]{3,2,1,0:T(8,128)}), f32[8,4,64,512]{3,2,1,0:T(8,128)}, u32[]{:S(2)}, u32[]{:S(2)}) async-start(f32[8,4,64,512]{3,2,1,0:T(8,128)} %bitcast.14), calls=%async_computation.2 | async-start | bytes 8388608 | tf_op jit(solution)/shard_map/all_to_all | solution.py:282
  239.9 69.6 %collective-permute-start.16 = (f32[32,64,128]{2,1,0:T(8,128)S(1)}, f32[32,64,128]{2,1,0:T(8,128)S(1)}, u32[]{:S(2)}, u32[]{:S(2)}) collective-permute-start(f32[32,64,128]{2,1,0:T(8,128)S(1)} %copy-done.17), channel_id=1, source_target_pairs={{0,2},{1,3},{2,0},{3,1},{4,6},{5,7},{6,4},{7,5},{8,10},{9,11},{10,... | collective-permute-start | bytes 3145736 | tf_op jit(solution)/shard_map/ppermute | solution.py:278
  241.2 68.3 %collective-permute-start.17 = (f32[32,64,128]{2,1,0:T(8,128)S(1)}, f32[32,64,128]{2,1,0:T(8,128)S(1)}, u32[]{:S(2)}, u32[]{:S(2)}) collective-permute-start(f32[32,64,128]{2,1,0:T(8,128)S(1)} %copy-done.16), channel_id=1, source_target_pairs={{0,3},{1,0},{2,1},{3,2},{4,7},{5,4},{6,5},{7,6},{8,11},{9,8},{10,9... | collective-permute-start | bytes 3145736 | tf_op jit(solution)/shard_map/ppermute | solution.py:278
  319.0 106.8 %all-to-all-start.4 = ((f32[8,4,64,512]{3,2,1,0:T(8,128)}), f32[8,4,64,512]{3,2,1,0:T(8,128)}, u32[]{:S(2)}, u32[]{:S(2)}) async-start(f32[8,4,64,512]{3,2,1,0:T(8,128)} %bitcast.13), calls=%async_computation.4 | async-start | bytes 8388608 | tf_op jit(solution)/shard_map/all_to_all | solution.py:282
  346.0 70.3 %collective-permute-start.28 = (f32[32,64,128]{2,1,0:T(8,128)S(1)}, f32[32,64,128]{2,1,0:T(8,128)S(1)}, u32[]{:S(2)}, u32[]{:S(2)}) collective-permute-start(f32[32,64,128]{2,1,0:T(8,128)S(1)} %copy-done.14), channel_id=1, source_target_pairs={{0,2},{1,3},{2,0},{3,1},{4,6},{5,7},{6,4},{7,5},{8,10},{9,11},{10,... | collective-permute-start | bytes 3145736 | tf_op jit(solution)/shard_map/ppermute | solution.py:278
  348.0 68.3 %collective-permute-start.29 = (f32[32,64,128]{2,1,0:T(8,128)S(1)}, f32[32,64,128]{2,1,0:T(8,128)S(1)}, u32[]{:S(2)}, u32[]{:S(2)}) collective-permute-start(f32[32,64,128]{2,1,0:T(8,128)S(1)} %copy-done.13), channel_id=1, source_target_pairs={{0,3},{1,0},{2,1},{3,2},{4,7},{5,4},{6,5},{7,6},{8,11},{9,8},{10,9... | collective-permute-start | bytes 3145736 | tf_op jit(solution)/shard_map/ppermute | solution.py:278
  637.5 130.5 %all-to-all-start.5 = ((f32[8,4,64,512]{3,2,1,0:T(8,128)}), f32[8,4,64,512]{3,2,1,0:T(8,128)}, u32[]{:S(2)}, u32[]{:S(2)}) async-start(f32[8,4,64,512]{3,2,1,0:T(8,128)} %solve_x.6), calls=%async_computation.5 | async-start | bytes 8388608 | tf_op jit(solution)/shard_map/all_to_all | solution.py:282
  674.8 70.0 %collective-permute-start.21 = (f32[32,64,128]{2,1,0:T(8,128)}, f32[32,64,128]{2,1,0:T(8,128)S(1)}, u32[]{:S(2)}, u32[]{:S(2)}) collective-permute-start(f32[32,64,128]{2,1,0:T(8,128)} %get-tuple-element.95), channel_id=1, source_target_pairs={{0,2},{1,3},{2,0},{3,1},{4,6},{5,7},{6,4},{7,5},{8,10},{9,11},{10,... | collective-permute-start | bytes 3145736 | tf_op jit(solution)/shard_map/ppermute | solution.py:278
  676.1 99.3 %collective-permute-start.24 = (f32[32,64,128]{2,1,0:T(8,128)}, f32[32,64,128]{2,1,0:T(8,128)S(1)}, u32[]{:S(2)}, u32[]{:S(2)}) collective-permute-start(f32[32,64,128]{2,1,0:T(8,128)} %get-tuple-element.98), channel_id=1, source_target_pairs={{0,3},{1,0},{2,1},{3,2},{4,7},{5,4},{6,5},{7,6},{8,11},{9,8},{10,9... | collective-permute-start | bytes 3145736 | tf_op jit(solution)/shard_map/ppermute | solution.py:278
  684.4 173.8 %collective-permute-start.19 = (f32[32,64,128]{2,1,0:T(8,128)}, f32[32,64,128]{2,1,0:T(8,128)}, u32[]{:S(2)}, u32[]{:S(2)}) collective-permute-start(f32[32,64,128]{2,1,0:T(8,128)} %get-tuple-element.93), channel_id=1, source_target_pairs={{0,1},{1,2},{2,3},{3,0},{4,5},{5,6},{6,7},{7,4},{8,9},{9,10},{10,1... | collective-permute-start | bytes 3145736 | tf_op jit(solution)/shard_map/ppermute | solution.py:278
  692.5 107.7 %collective-permute-start.39 = (f32[32,16,128]{2,1,0:T(8,128)}, f32[32,16,128]{2,1,0:T(8,128)S(1)}, u32[]{:S(2)}, u32[]{:S(2)}) collective-permute-start(f32[32,16,128]{2,1,0:T(8,128)} %get-tuple-element.118), channel_id=1, source_target_pairs={{0,1},{1,2},{2,3},{3,0},{4,5},{5,6},{6,7},{7,4},{8,9},{9,10},{10,1... | collective-permute-start | bytes 786440 | tf_op jit(solution)/shard_map/ppermute | solution.py:278
  699.5 129.5 %collective-permute-start.40 = (f32[32,16,128]{2,1,0:T(8,128)}, f32[32,16,128]{2,1,0:T(8,128)}, u32[]{:S(2)}, u32[]{:S(2)}) collective-permute-start(f32[32,16,128]{2,1,0:T(8,128)} %get-tuple-element.119), channel_id=1, source_target_pairs={{0,2},{1,3},{2,0},{3,1},{4,6},{5,7},{6,4},{7,5},{8,10},{9,11},{10,... | collective-permute-start | bytes 786440 | tf_op jit(solution)/shard_map/ppermute | solution.py:278
  744.8 110.3 %collective-permute-start.41 = (f32[32,16,128]{2,1,0:T(8,128)}, f32[32,16,128]{2,1,0:T(8,128)}, u32[]{:S(2)}, u32[]{:S(2)}) collective-permute-start(f32[32,16,128]{2,1,0:T(8,128)} %get-tuple-element.120), channel_id=1, source_target_pairs={{0,3},{1,0},{2,1},{3,2},{4,7},{5,4},{6,5},{7,6},{8,11},{9,8},{10,9... | collective-permute-start | bytes 786440 | tf_op jit(solution)/shard_map/ppermute | solution.py:278
  775.5 85.7 %collective-permute-start.22 = (f32[32,64,128]{2,1,0:T(8,128)}, f32[32,64,128]{2,1,0:T(8,128)S(1)}, u32[]{:S(2)}, u32[]{:S(2)}) collective-permute-start(f32[32,64,128]{2,1,0:T(8,128)} %get-tuple-element.96), channel_id=1, source_target_pairs={{0,2},{1,3},{2,0},{3,1},{4,6},{5,7},{6,4},{7,5},{8,10},{9,11},{10,... | collective-permute-start | bytes 3145736 | tf_op jit(solution)/shard_map/ppermute | solution.py:278
  800.2 101.7 %collective-permute-start.25 = (f32[32,64,128]{2,1,0:T(8,128)}, f32[32,64,128]{2,1,0:T(8,128)S(1)}, u32[]{:S(2)}, u32[]{:S(2)}) collective-permute-start(f32[32,64,128]{2,1,0:T(8,128)} %get-tuple-element.99), channel_id=1, source_target_pairs={{0,3},{1,0},{2,1},{3,2},{4,7},{5,4},{6,5},{7,6},{8,11},{9,8},{10,9... | collective-permute-start | bytes 3145736 | tf_op jit(solution)/shard_map/ppermute | solution.py:278
  829.0 94.8 %collective-permute-start.20 = (f32[32,64,128]{2,1,0:T(8,128)}, f32[32,64,128]{2,1,0:T(8,128)}, u32[]{:S(2)}, u32[]{:S(2)}) collective-permute-start(f32[32,64,128]{2,1,0:T(8,128)} %get-tuple-element.94), channel_id=1, source_target_pairs={{0,1},{1,2},{2,3},{3,0},{4,5},{5,6},{6,7},{7,4},{8,9},{9,10},{10,1... | collective-permute-start | bytes 3145736 | tf_op jit(solution)/shard_map/ppermute | solution.py:278
  855.1 108.7 %collective-permute-start.23 = (f32[32,64,128]{2,1,0:T(8,128)}, f32[32,64,128]{2,1,0:T(8,128)}, u32[]{:S(2)}, u32[]{:S(2)}) collective-permute-start(f32[32,64,128]{2,1,0:T(8,128)} %get-tuple-element.97), channel_id=1, source_target_pairs={{0,2},{1,3},{2,0},{3,1},{4,6},{5,7},{6,4},{7,5},{8,10},{9,11},{10,... | collective-permute-start | bytes 3145736 | tf_op jit(solution)/shard_map/ppermute | solution.py:278
  858.2 105.6 %collective-permute-start.26 = (f32[32,64,128]{2,1,0:T(8,128)}, f32[32,64,128]{2,1,0:T(8,128)}, u32[]{:S(2)}, u32[]{:S(2)}) collective-permute-start(f32[32,64,128]{2,1,0:T(8,128)} %get-tuple-element.100), channel_id=1, source_target_pairs={{0,3},{1,0},{2,1},{3,2},{4,7},{5,4},{6,5},{7,6},{8,11},{9,8},{10,9... | collective-permute-start | bytes 3145736 | tf_op jit(solution)/shard_map/ppermute | solution.py:278
  861.1 179.5 %collective-permute-start.30 = (f32[32,16,128]{2,1,0:T(8,128)}, f32[32,16,128]{2,1,0:T(8,128)S(1)}, u32[]{:S(2)}, u32[]{:S(2)}) collective-permute-start(f32[32,16,128]{2,1,0:T(8,128)} %get-tuple-element.106), channel_id=1, source_target_pairs={{0,1},{1,2},{2,3},{3,0},{4,5},{5,6},{6,7},{7,4},{8,9},{9,10},{10,1... | collective-permute-start | bytes 786440 | tf_op jit(solution)/shard_map/ppermute | solution.py:278
  901.9 138.7 %collective-permute-start.31 = (f32[32,16,128]{2,1,0:T(8,128)}, f32[32,16,128]{2,1,0:T(8,128)}, u32[]{:S(2)}, u32[]{:S(2)}) collective-permute-start(f32[32,16,128]{2,1,0:T(8,128)} %get-tuple-element.107), channel_id=1, source_target_pairs={{0,2},{1,3},{2,0},{3,1},{4,6},{5,7},{6,4},{7,5},{8,10},{9,11},{10,... | collective-permute-start | bytes 786440 | tf_op jit(solution)/shard_map/ppermute | solution.py:278
  923.8 66.5 %collective-permute-start.36 = (f32[32,16,128]{2,1,0:T(8,128)}, f32[32,16,128]{2,1,0:T(8,128)}, u32[]{:S(2)}, u32[]{:S(2)}) collective-permute-start(f32[32,16,128]{2,1,0:T(8,128)} %get-tuple-element.114), channel_id=1, source_target_pairs={{0,1},{1,2},{2,3},{3,0},{4,5},{5,6},{6,7},{7,4},{8,9},{9,10},{10,1... | collective-permute-start | bytes 786440 | tf_op jit(solution)/shard_map/ppermute | solution.py:278
  (70 other events, 2111.6 us)

commit v2 on v1

--- a/solution.py
+++ b/solution.py
@@ -159,8 +159,9 @@
 
 def forward_y(basis, fields, me):
     count, pieces = len(fields), len(fields[0])
-    planes, piece, width = fields[0][0].shape
-    lines = piece * pieces
+    planes, _, width = fields[0][0].shape
+    sizes = [part.shape[1] for part in fields[0]]
+    lines = sum(sizes)
     full = basis.shape[1]
     step, grid = y_grid(planes, lines)
 
@@ -185,7 +186,7 @@
         kernel,
         grid=grid,
         in_specs=[smem(), whole(basis.shape)]
-        + [pl.BlockSpec((step, piece, width), lambda i: (i, 0, 0))] * (count * pieces),
+        + [pl.BlockSpec((step, size, width), lambda i: (i, 0, 0)) for size in sizes] * count,
         out_specs=pl.BlockSpec((step, lines, full), lambda i: (i, 0, 0)),
         out_shape=jax.ShapeDtypeStruct((planes, lines, full), F32),
         scratch_shapes=[pltpu.VMEM((count * width, full), BF16)] * 2,
@@ -194,10 +195,10 @@
     )(me, basis, *[part for parts in fields for part in parts])
 
 
-def backward_y(basis, field, me, count, pieces):
+def backward_y(basis, field, me, count, sizes):
     planes, lines, full = field.shape
     width = basis.shape[0] // count
-    piece = lines // pieces
+    edges = [sum(sizes[:at]) for at in range(len(sizes))]
     step, grid = y_grid(planes, lines)
 
     def kernel(me_ref, basis_ref, field_ref, *refs):
@@ -214,15 +215,15 @@
         result = product(halves(field), (high[...], low[...]), ((1,), (1,)))
         for shift in range(count):
             block = result[:, shift * width : (shift + 1) * width].reshape(step, lines, width)
-            for at in range(pieces):
-                outs[at * count + shift][...] = block[:, at * piece : (at + 1) * piece]
+            for at, edge in enumerate(edges):
+                outs[at * count + shift][...] = block[:, edge : edge + sizes[at]]
 
     return pl.pallas_call(
         kernel,
         grid=grid,
         in_specs=[smem(), whole(basis.shape), pl.BlockSpec((step, lines, full), lambda i: (i, 0, 0))],
-        out_specs=[pl.BlockSpec((step, piece, width), lambda i: (i, 0, 0))] * (count * pieces),
-        out_shape=[jax.ShapeDtypeStruct((planes, piece, width), F32)] * (count * pieces),
+        out_specs=[pl.BlockSpec((step, size, width), lambda i: (i, 0, 0)) for size in sizes for _ in range(count)],
+        out_shape=[jax.ShapeDtypeStruct((planes, size, width), F32) for size in sizes for _ in range(count)],
         scratch_shapes=[pltpu.VMEM((count * width, full), BF16)] * 2,
         cost_estimate=cost(2 * planes * lines * width * count * full, planes * lines * (width * count + full)),
         name="backward_y",
@@ -258,6 +259,24 @@
         cost_estimate=cost(4 * planes * nx * nx * full, 2 * planes * nx * full),
         name="solve_x",
     )(eigen_z, basis, eigen_x[:, None], eigen_y[None, :], field)
+
+
+def piece_sizes(lines):
+    units = max(1, lines // LINES)
+    count = min(PARTS, units)
+    sizes = [units // count] * count
+    sizes[-1] += units - sum(sizes)
+    if sizes[0] > 1:
+        sizes[0], sizes[-1] = sizes[0] - 1, sizes[-1] + 1
+    return [size * (lines // units) for size in sizes]
+
+
+def last_sizes(lines):
+    count = max(1, min(PARTS, lines // LINES))
+    sizes = [lines // count] * count
+    if sizes[-1] >= 2 * LINES:
+        sizes[-1:] = [sizes[-1] - LINES, LINES]
+    return sizes
 
 
 def local(source, basis_x, basis_y, basis_z, eigen_x, eigen_y, eigen_z):
@@ -281,11 +300,11 @@
     def along_row(field):
         return lax.all_to_all(field, "row", split_axis=0, concat_axis=0, tiled=True)
 
-    pieces = max(1, min(PARTS, lines // LINES))
-    piece = lines // pieces
+    sizes = piece_sizes(lines)
+    ends = last_sizes(lines)
     first = []
-    for at in range(pieces):
-        sent = forward_z(basis_z, source, me, cols, planes, [0], at * piece, piece)
+    for at, size in enumerate(sizes):
+        sent = forward_z(basis_z, source, me, cols, planes, [0], sum(sizes[:at]), size)
         first.append(along_col(sent))
     got = [[[part[shift] for part in first] for shift in range(cols)]]
     if chunks > 1:
@@ -302,15 +321,16 @@
         field = along_row(field)
         field = field.reshape(planes, lines, field.shape[3])
         final = chunk == chunks - 1
-        sent = backward_y(basis_y, field, me, cols, pieces if final else 1)
+        sent = backward_y(basis_y, field, me, cols, ends if final else [lines])
         if not final:
             back.append(along_col(sent))
     fields = [moved[shift] for shift in range(cols) for moved in back]
     result = None
     ready = prepare_z(basis_z, me, cols)
-    last = [along_col(sent[at * cols : (at + 1) * cols]) for at in range(pieces)]
-    for at in range(pieces):
-        result = backward_z(ready, fields, last[at], cols, lines, at * piece, result)
+    last = [along_col(sent[at * cols : (at + 1) * cols]) for at in range(len(ends))]
+    for at in range(len(ends)):
+        edge = sum(ends[:at])
+        result = backward_z(ready, fields, last[at], cols, lines, edge, result)
     return result
 
 

time: 1050 us -> 1060 us (level)
    ppermute x42 -> x45, starting transfers between devices: 291 us -> 288 us  [along_col(): moved.append(lax.ppermute(fields[shift], 'col', ring))]
    pallas_call x4 -> x5, Pallas kernels: 34.7 us -> 37.7 us  [backward_z(): pl.pallas_call(kernel, grid=(lines // step,), in_specs=[whole((depth, ful...]
    ppermute x42 -> x45, waiting for transfers between devices: 376 us -> 375 us  [along_col(): moved.append(lax.ppermute(fields[shift], 'col', ring))]
  transfers between devices with their start and end apart: 50 -> 53, of which waited for: 22 -> 17; matrix products, arithmetic and copies ran while one was open for 0% -> 0% of each run, Pallas kernels for 15% -> 16%
where the time goes in v2:
time: 1060 us; the launch traced here: 1050 us
  waiting for transfers between devices  512 us (48%)
  starting transfers between devices  343 us (32%)
  Pallas kernels  186 us (18%)
    ppermute x45, waiting for transfers between devices, along_col(): moved.append(lax.ppermute(fields[shift], 'col', ring))  375 us
    ppermute x45, starting transfers between devices, along_col(): moved.append(lax.ppermute(fields[shift], 'col', ring))  288 us
    all_to_all x8, waiting for transfers between devices, along_row(): return lax.all_to_all(field, 'row', split_axis=0, concat_axis=0, tiled=True)  138 us
    all_to_all x8, starting transfers between devices, along_row(): return lax.all_to_all(field, 'row', split_axis=0, concat_axis=0, tiled=True)  54.8 us
    pallas_call x4, Pallas kernels, solve_x(): pl.pallas_call(kernel, grid=(planes,), in_specs=[smem(), whole((nx, nx)),...  43.2 us
    pallas_call x5, Pallas kernels, forward_z(): pl.pallas_call(kernel, grid=(lines // step,), in_specs=[smem(), whole((de...  42.3 us
    pallas_call x5, Pallas kernels, backward_z(): pl.pallas_call(kernel, grid=(lines // step,), in_specs=[whole((depth, ful...  37.7 us
    pallas_call x4, Pallas kernels, backward_y(): pl.pallas_call(kernel, grid=grid, in_specs=[smem(), whole(basis.shape), p...  29.9 us
  transfers between devices with their start and end apart: 53, of which 17 were waited for; matrix products, arithmetic and copies ran while one was open for 0% of the time, Pallas kernels for 16%

profile of v2, /device:TPU:1, one launch (start us, length us, event | category | flops | bytes accessed | tf_op | source)
XLA Modules:
  0.0 1052.0 jit_solution(4780123934050874323)
XLA Ops:
  43.9 20.7 %collective-permute-start.5 = (f32[32,16,128]{2,1,0:T(8,128)S(1)}, f32[32,16,128]{2,1,0:T(8,128)S(1)}, u32[]{:S(2)}, u32[]{:S(2)}) collective-permute-start(f32[32,16,128]{2,1,0:T(8,128)S(1)} %copy-done.39), channel_id=1, source_target_pairs={{0,2},{1,3},{2,0},{3,1},{4,6},{5,7},{6,4},{7,5},{8,10},{9,11},{10,... | collective-permute-start | bytes 786440 | tf_op jit(solution)/shard_map/ppermute | solution.py:297
  67.8 25.7 %collective-permute-done.5.refs_9_ = f32[32,16,128]{2,1,0:T(8,128)S(1)} collective-permute-done((f32[32,16,128]{2,1,0:T(8,128)S(1)}, f32[32,16,128]{2,1,0:T(8,128)S(1)}, u32[]{:S(2)}, u32[]{:S(2)}) %collective-permute-start.5) | collective-permute-done | bytes 262176 | tf_op jit(solution)/shard_map/ppermute | solution.py:297
  108.9 18.9 %forward_z.9 = (f32[32,64,128]{2,1,0:T(8,128)}, f32[32,64,128]{2,1,0:T(8,128)}, f32[32,64,128]{2,1,0:T(8,128)}, f32[32,64,128]{2,1,0:T(8,128)}, f32[32,64,128]{2...) custom-call(s32[1]{0:T(128)} %bitcast.me_ref, ...), custom_call_target="tpu_custom_call" | custom-call | flops 9663676416 | bytes 29360128 | tf_op jit(solution)/shard_map/forward_z/pallas_call | solution.py:73
  134.9 22.6 %collective-permute-done.12.refs_1_ = f32[32,64,128]{2,1,0:T(8,128)S(1)} collective-permute-done((f32[32,64,128]{2,1,0:T(8,128)}, f32[32,64,128]{2,1,0:T(8,128)S(1)}, u32[]{:S(2)}, u32[]{:S(2)}) %collective-permute-start.12) | collective-permute-done | bytes 1048608 | tf_op jit(solution)/shard_map/ppermute | solution.py:297
  157.5 45.1 %collective-permute-done.13.refs_2_ = f32[32,64,128]{2,1,0:T(8,128)S(1)} collective-permute-done((f32[32,64,128]{2,1,0:T(8,128)}, f32[32,64,128]{2,1,0:T(8,128)S(1)}, u32[]{:S(2)}, u32[]{:S(2)}) %collective-permute-start.13) | collective-permute-done | bytes 1048608 | tf_op jit(solution)/shard_map/ppermute | solution.py:297
  216.7 22.3 %collective-permute-start.15 = (f32[32,64,128]{2,1,0:T(8,128)S(1)}, f32[32,64,128]{2,1,0:T(8,128)S(1)}, u32[]{:S(2)}, u32[]{:S(2)}) collective-permute-start(f32[32,64,128]{2,1,0:T(8,128)S(1)} %copy-done.20), channel_id=1, source_target_pairs={{0,1},{1,2},{2,3},{3,0},{4,5},{5,6},{6,7},{7,4},{8,9},{9,10},{10,1... | collective-permute-start | bytes 3145736 | tf_op jit(solution)/shard_map/ppermute | solution.py:297
  241.2 22.3 %collective-permute-done.15.refs_1_ = f32[32,64,128]{2,1,0:T(8,128)S(1)} collective-permute-done((f32[32,64,128]{2,1,0:T(8,128)S(1)}, f32[32,64,128]{2,1,0:T(8,128)S(1)}, u32[]{:S(2)}, u32[]{:S(2)}) %collective-permute-start.15) | collective-permute-done | bytes 1048608 | tf_op jit(solution)/shard_map/ppermute | solution.py:297
  263.4 45.2 %collective-permute-done.16.refs_2_ = f32[32,64,128]{2,1,0:T(8,128)S(1)} collective-permute-done((f32[32,64,128]{2,1,0:T(8,128)S(1)}, f32[32,64,128]{2,1,0:T(8,128)S(1)}, u32[]{:S(2)}, u32[]{:S(2)}) %collective-permute-start.16) | collective-permute-done | bytes 1048608 | tf_op jit(solution)/shard_map/ppermute | solution.py:297
  323.3 21.7 %collective-permute-start.27 = (f32[32,64,128]{2,1,0:T(8,128)S(1)}, f32[32,64,128]{2,1,0:T(8,128)S(1)}, u32[]{:S(2)}, u32[]{:S(2)}) collective-permute-start(f32[32,64,128]{2,1,0:T(8,128)S(1)} %copy-done.17), channel_id=1, source_target_pairs={{0,1},{1,2},{2,3},{3,0},{4,5},{5,6},{6,7},{7,4},{8,9},{9,10},{10,1... | collective-permute-start | bytes 3145736 | tf_op jit(solution)/shard_map/ppermute | solution.py:297
  347.2 23.0 %collective-permute-done.27.refs_1_ = f32[32,64,128]{2,1,0:T(8,128)S(1)} collective-permute-done((f32[32,64,128]{2,1,0:T(8,128)S(1)}, f32[32,64,128]{2,1,0:T(8,128)S(1)}, u32[]{:S(2)}, u32[]{:S(2)}) %collective-permute-start.27) | collective-permute-done | bytes 1048608 | tf_op jit(solution)/shard_map/ppermute | solution.py:297
  370.2 45.2 %collective-permute-done.28.refs_2_ = f32[32,64,128]{2,1,0:T(8,128)S(1)} collective-permute-done((f32[32,64,128]{2,1,0:T(8,128)S(1)}, f32[32,64,128]{2,1,0:T(8,128)S(1)}, u32[]{:S(2)}, u32[]{:S(2)}) %collective-permute-start.28) | collective-permute-done | bytes 1048608 | tf_op jit(solution)/shard_map/ppermute | solution.py:297
  442.2 33.1 %all-to-all-done.6.in_ref = f32[8,4,64,512]{3,2,1,0:T(8,128)} async-done(((f32[8,4,64,512]{3,2,1,0:T(8,128)}), f32[8,4,64,512]{3,2,1,0:T(8,128)}, u32[]{:S(2)}, u32[]{:S(2)}) %all-to-all-start.6) | async-done | bytes 4194336 | tf_op jit(solution)/shard_map/all_to_all | solution.py:301
  494.4 34.8 %all-to-all-done.1 = f32[8,4,64,512]{3,2,1,0:T(8,128)} async-done(((f32[8,4,64,512]{3,2,1,0:T(8,128)}), f32[8,4,64,512]{3,2,1,0:T(8,128)}, u32[]{:S(2)}, u32[]{:S(2)}) %all-to-all-start.1) | async-done | bytes 4194336 | tf_op jit(solution)/shard_map/all_to_all | solution.py:301
  548.1 34.8 %all-to-all-done.3 = f32[8,4,64,512]{3,2,1,0:T(8,128)} async-done(((f32[8,4,64,512]{3,2,1,0:T(8,128)}), f32[8,4,64,512]{3,2,1,0:T(8,128)}, u32[]{:S(2)}, u32[]{:S(2)}) %all-to-all-start.3) | async-done | bytes 4194336 | tf_op jit(solution)/shard_map/all_to_all | solution.py:301
  601.7 34.8 %all-to-all-done.7 = f32[8,4,64,512]{3,2,1,0:T(8,128)} async-done(((f32[8,4,64,512]{3,2,1,0:T(8,128)}), f32[8,4,64,512]{3,2,1,0:T(8,128)}, u32[]{:S(2)}, u32[]{:S(2)}) %all-to-all-start.7) | async-done | bytes 4194336 | tf_op jit(solution)/shard_map/all_to_all | solution.py:301
  652.0 21.7 %collective-permute-start.18 = (f32[32,64,128]{2,1,0:T(8,128)}, f32[32,64,128]{2,1,0:T(8,128)S(1)}, u32[]{:S(2)}, u32[]{:S(2)}) collective-permute-start(f32[32,64,128]{2,1,0:T(8,128)} %get-tuple-element.96), channel_id=1, source_target_pairs={{0,1},{1,2},{2,3},{3,0},{4,5},{5,6},{6,7},{7,4},{8,9},{9,10},{10,1... | collective-permute-start | bytes 3145736 | tf_op jit(solution)/shard_map/ppermute | solution.py:297
  691.6 79.9 %collective-permute-done.42.refs_13_ = f32[32,16,128]{2,1,0:T(8,128)S(1)} collective-permute-done((f32[32,16,128]{2,1,0:T(8,128)}, f32[32,16,128]{2,1,0:T(8,128)S(1)}, u32[]{:S(2)}, u32[]{:S(2)}) %collective-permute-start.42) | collective-permute-done | bytes 262176 | tf_op jit(solution)/shard_map/ppermute | solution.py:297
  771.5 22.5 %collective-permute-start.43 = (f32[32,16,128]{2,1,0:T(8,128)}, f32[32,16,128]{2,1,0:T(8,128)}, u32[]{:S(2)}, u32[]{:S(2)}) collective-permute-start(f32[32,16,128]{2,1,0:T(8,128)} %get-tuple-element.127), channel_id=1, source_target_pairs={{0,2},{1,3},{2,0},{3,1},{4,6},{5,7},{6,4},{7,5},{8,10},{9,11},{10,... | collective-permute-start | bytes 786440 | tf_op jit(solution)/shard_map/ppermute | solution.py:297
  794.0 12.4 %collective-permute-done.43.refs_14_ = f32[32,16,128]{2,1,0:T(8,128)} collective-permute-done((f32[32,16,128]{2,1,0:T(8,128)}, f32[32,16,128]{2,1,0:T(8,128)}, u32[]{:S(2)}, u32[]{:S(2)}) %collective-permute-start.43) | collective-permute-done | bytes 262176 | tf_op jit(solution)/shard_map/ppermute | solution.py:297
  823.8 37.9 %collective-permute-done.22.refs_7_ = f32[32,64,128]{2,1,0:T(8,128)} collective-permute-done((f32[32,64,128]{2,1,0:T(8,128)}, f32[32,64,128]{2,1,0:T(8,128)}, u32[]{:S(2)}, u32[]{:S(2)}) %collective-permute-start.22) | collective-permute-done | bytes 1048608 | tf_op jit(solution)/shard_map/ppermute | solution.py:297
  861.7 22.7 %collective-permute-start.30 = (f32[32,8,128]{2,1,0:T(8,128)}, f32[32,8,128]{2,1,0:T(8,128)S(1)}, u32[]{:S(2)}, u32[]{:S(2)}) collective-permute-start(f32[32,8,128]{2,1,0:T(8,128)} %get-tuple-element.110), channel_id=1, source_target_pairs={{0,1},{1,2},{2,3},{3,0},{4,5},{5,6},{6,7},{7,4},{8,9},{9,10},{10,1... | collective-permute-start | bytes 393224 | tf_op jit(solution)/shard_map/ppermute | solution.py:297
  884.4 44.0 %collective-permute-start.31 = (f32[32,8,128]{2,1,0:T(8,128)}, f32[32,8,128]{2,1,0:T(8,128)}, u32[]{:S(2)}, u32[]{:S(2)}) collective-permute-start(f32[32,8,128]{2,1,0:T(8,128)} %get-tuple-element.111), channel_id=1, source_target_pairs={{0,2},{1,3},{2,0},{3,1},{4,6},{5,7},{6,4},{7,5},{8,10},{9,11},{10,... | collective-permute-start | bytes 393224 | tf_op jit(solution)/shard_map/ppermute | solution.py:297
  928.4 25.2 %collective-permute-start.39 = (f32[32,16,128]{2,1,0:T(8,128)}, f32[32,16,128]{2,1,0:T(8,128)S(1)}, u32[]{:S(2)}, u32[]{:S(2)}) collective-permute-start(f32[32,16,128]{2,1,0:T(8,128)} %get-tuple-element.122), channel_id=1, source_target_pairs={{0,1},{1,2},{2,3},{3,0},{4,5},{5,6},{6,7},{7,4},{8,9},{9,10},{10,1... | collective-permute-start | bytes 786440 | tf_op jit(solution)/shard_map/ppermute | solution.py:297
  962.8 21.7 %collective-permute-start.41 = (f32[32,16,128]{2,1,0:T(8,128)}, f32[32,16,128]{2,1,0:T(8,128)}, u32[]{:S(2)}, u32[]{:S(2)}) collective-permute-start(f32[32,16,128]{2,1,0:T(8,128)} %get-tuple-element.124), channel_id=1, source_target_pairs={{0,3},{1,0},{2,1},{3,2},{4,7},{5,4},{6,5},{7,6},{8,11},{9,8},{10,9... | collective-permute-start | bytes 786440 | tf_op jit(solution)/shard_map/ppermute | solution.py:297
  (207 shorter events, 313.3 us)
Async XLA Ops:
  32.8 60.7 %collective-permute-start.3 = (f32[32,24,128]{2,1,0:T(8,128)}, f32[32,24,128]{2,1,0:T(8,128)S(1)}, u32[]{:S(2)}, u32[]{:S(2)}) collective-permute-start(f32[32,24,128]{2,1,0:T(8,128)} %get-tuple-element.76), channel_id=1, source_target_pairs={{0,1},{1,2},{2,3},{3,0},{4,5},{5,6},{6,7},{7,4},{8,9},{9,10},{10,1... | collective-permute-start | bytes 1179656 | tf_op jit(solution)/shard_map/ppermute | solution.py:297
  37.5 55.9 %collective-permute-start.7 = (f32[32,24,128]{2,1,0:T(8,128)}, f32[32,24,128]{2,1,0:T(8,128)S(1)}, u32[]{:S(2)}, u32[]{:S(2)}) collective-permute-start(f32[32,24,128]{2,1,0:T(8,128)} %get-tuple-element.80), channel_id=1, source_target_pairs={{0,2},{1,3},{2,0},{3,1},{4,6},{5,7},{6,4},{7,5},{8,10},{9,11},{10,... | collective-permute-start | bytes 1179656 | tf_op jit(solution)/shard_map/ppermute | solution.py:297
  102.2 109.2 %all-to-all-start = ((f32[8,4,64,512]{3,2,1,0:T(8,128)}), f32[8,4,64,512]{3,2,1,0:T(8,128)}, u32[]{:S(2)}, u32[]{:S(2)}) async-start(f32[8,4,64,512]{3,2,1,0:T(8,128)} %bitcast.12), calls=%async_computation | async-start | bytes 8388608 | tf_op jit(solution)/shard_map/all_to_all | solution.py:301
  132.7 69.9 %collective-permute-start.13 = (f32[32,64,128]{2,1,0:T(8,128)}, f32[32,64,128]{2,1,0:T(8,128)S(1)}, u32[]{:S(2)}, u32[]{:S(2)}) collective-permute-start(f32[32,64,128]{2,1,0:T(8,128)} %get-tuple-element.88), channel_id=1, source_target_pairs={{0,2},{1,3},{2,0},{3,1},{4,6},{5,7},{6,4},{7,5},{8,10},{9,11},{10,... | collective-permute-start | bytes 3145736 | tf_op jit(solution)/shard_map/ppermute | solution.py:297
  134.1 68.5 %collective-permute-start.14 = (f32[32,64,128]{2,1,0:T(8,128)}, f32[32,64,128]{2,1,0:T(8,128)S(1)}, u32[]{:S(2)}, u32[]{:S(2)}) collective-permute-start(f32[32,64,128]{2,1,0:T(8,128)} %get-tuple-element.89), channel_id=1, source_target_pairs={{0,3},{1,0},{2,1},{3,2},{4,7},{5,4},{6,5},{7,6},{8,11},{9,8},{10,9... | collective-permute-start | bytes 3145736 | tf_op jit(solution)/shard_map/ppermute | solution.py:297
  211.4 106.6 %all-to-all-start.2 = ((f32[8,4,64,512]{3,2,1,0:T(8,128)}), f32[8,4,64,512]{3,2,1,0:T(8,128)}, u32[]{:S(2)}, u32[]{:S(2)}) async-start(f32[8,4,64,512]{3,2,1,0:T(8,128)} %bitcast.14), calls=%async_computation.2 | async-start | bytes 8388608 | tf_op jit(solution)/shard_map/all_to_all | solution.py:301
  239.0 69.6 %collective-permute-start.16 = (f32[32,64,128]{2,1,0:T(8,128)S(1)}, f32[32,64,128]{2,1,0:T(8,128)S(1)}, u32[]{:S(2)}, u32[]{:S(2)}) collective-permute-start(f32[32,64,128]{2,1,0:T(8,128)S(1)} %copy-done.19), channel_id=1, source_target_pairs={{0,2},{1,3},{2,0},{3,1},{4,6},{5,7},{6,4},{7,5},{8,10},{9,11},{10,... | collective-permute-start | bytes 3145736 | tf_op jit(solution)/shard_map/ppermute | solution.py:297
  240.3 68.3 %collective-permute-start.17 = (f32[32,64,128]{2,1,0:T(8,128)S(1)}, f32[32,64,128]{2,1,0:T(8,128)S(1)}, u32[]{:S(2)}, u32[]{:S(2)}) collective-permute-start(f32[32,64,128]{2,1,0:T(8,128)S(1)} %copy-done.18), channel_id=1, source_target_pairs={{0,3},{1,0},{2,1},{3,2},{4,7},{5,4},{6,5},{7,6},{8,11},{9,8},{10,9... | collective-permute-start | bytes 3145736 | tf_op jit(solution)/shard_map/ppermute | solution.py:297
  318.0 106.7 %all-to-all-start.4 = ((f32[8,4,64,512]{3,2,1,0:T(8,128)}), f32[8,4,64,512]{3,2,1,0:T(8,128)}, u32[]{:S(2)}, u32[]{:S(2)}) async-start(f32[8,4,64,512]{3,2,1,0:T(8,128)} %bitcast.13), calls=%async_computation.4 | async-start | bytes 8388608 | tf_op jit(solution)/shard_map/all_to_all | solution.py:301
  345.0 70.3 %collective-permute-start.28 = (f32[32,64,128]{2,1,0:T(8,128)S(1)}, f32[32,64,128]{2,1,0:T(8,128)S(1)}, u32[]{:S(2)}, u32[]{:S(2)}) collective-permute-start(f32[32,64,128]{2,1,0:T(8,128)S(1)} %copy-done.16), channel_id=1, source_target_pairs={{0,2},{1,3},{2,0},{3,1},{4,6},{5,7},{6,4},{7,5},{8,10},{9,11},{10,... | collective-permute-start | bytes 3145736 | tf_op jit(solution)/shard_map/ppermute | solution.py:297
  347.0 68.3 %collective-permute-start.29 = (f32[32,64,128]{2,1,0:T(8,128)S(1)}, f32[32,64,128]{2,1,0:T(8,128)S(1)}, u32[]{:S(2)}, u32[]{:S(2)}) collective-permute-start(f32[32,64,128]{2,1,0:T(8,128)S(1)} %copy-done.15), channel_id=1, source_target_pairs={{0,3},{1,0},{2,1},{3,2},{4,7},{5,4},{6,5},{7,6},{8,11},{9,8},{10,9... | collective-permute-start | bytes 3145736 | tf_op jit(solution)/shard_map/ppermute | solution.py:297
  636.5 169.9 %all-to-all-start.5 = ((f32[8,4,64,512]{3,2,1,0:T(8,128)}), f32[8,4,64,512]{3,2,1,0:T(8,128)}, u32[]{:S(2)}, u32[]{:S(2)}) async-start(f32[8,4,64,512]{3,2,1,0:T(8,128)} %solve_x.6), calls=%async_computation.5 | async-start | bytes 8388608 | tf_op jit(solution)/shard_map/all_to_all | solution.py:301
  652.0 162.0 %collective-permute-start.18 = (f32[32,64,128]{2,1,0:T(8,128)}, f32[32,64,128]{2,1,0:T(8,128)S(1)}, u32[]{:S(2)}, u32[]{:S(2)}) collective-permute-start(f32[32,64,128]{2,1,0:T(8,128)} %get-tuple-element.96), channel_id=1, source_target_pairs={{0,1},{1,2},{2,3},{3,0},{4,5},{5,6},{6,7},{7,4},{8,9},{9,10},{10,1... | collective-permute-start | bytes 3145736 | tf_op jit(solution)/shard_map/ppermute | solution.py:297
  673.7 143.8 %collective-permute-start.21 = (f32[32,64,128]{2,1,0:T(8,128)}, f32[32,64,128]{2,1,0:T(8,128)S(1)}, u32[]{:S(2)}, u32[]{:S(2)}) collective-permute-start(f32[32,64,128]{2,1,0:T(8,128)} %get-tuple-element.99), channel_id=1, source_target_pairs={{0,2},{1,3},{2,0},{3,1},{4,6},{5,7},{6,4},{7,5},{8,10},{9,11},{10,... | collective-permute-start | bytes 3145736 | tf_op jit(solution)/shard_map/ppermute | solution.py:297
  675.0 142.5 %collective-permute-start.24 = (f32[32,64,128]{2,1,0:T(8,128)}, f32[32,64,128]{2,1,0:T(8,128)S(1)}, u32[]{:S(2)}, u32[]{:S(2)}) collective-permute-start(f32[32,64,128]{2,1,0:T(8,128)} %get-tuple-element.102), channel_id=1, source_target_pairs={{0,3},{1,0},{2,1},{3,2},{4,7},{5,4},{6,5},{7,6},{8,11},{9,8},{10,9... | collective-permute-start | bytes 3145736 | tf_op jit(solution)/shard_map/ppermute | solution.py:297
  683.3 134.6 %collective-permute-start.19 = (f32[32,64,128]{2,1,0:T(8,128)}, f32[32,64,128]{2,1,0:T(8,128)}, u32[]{:S(2)}, u32[]{:S(2)}) collective-permute-start(f32[32,64,128]{2,1,0:T(8,128)} %get-tuple-element.97), channel_id=1, source_target_pairs={{0,1},{1,2},{2,3},{3,0},{4,5},{5,6},{6,7},{7,4},{8,9},{9,10},{10,1... | collective-permute-start | bytes 3145736 | tf_op jit(solution)/shard_map/ppermute | solution.py:297
  691.5 80.0 %collective-permute-start.42 = (f32[32,16,128]{2,1,0:T(8,128)}, f32[32,16,128]{2,1,0:T(8,128)S(1)}, u32[]{:S(2)}, u32[]{:S(2)}) collective-permute-start(f32[32,16,128]{2,1,0:T(8,128)} %get-tuple-element.126), channel_id=1, source_target_pairs={{0,1},{1,2},{2,3},{3,0},{4,5},{5,6},{6,7},{7,4},{8,9},{9,10},{10,1... | collective-permute-start | bytes 786440 | tf_op jit(solution)/shard_map/ppermute | solution.py:297
  814.0 70.4 %collective-permute-start.25 = (f32[32,64,128]{2,1,0:T(8,128)}, f32[32,64,128]{2,1,0:T(8,128)}, u32[]{:S(2)}, u32[]{:S(2)}) collective-permute-start(f32[32,64,128]{2,1,0:T(8,128)} %get-tuple-element.103), channel_id=1, source_target_pairs={{0,3},{1,0},{2,1},{3,2},{4,7},{5,4},{6,5},{7,6},{8,11},{9,8},{10,9... | collective-permute-start | bytes 3145736 | tf_op jit(solution)/shard_map/ppermute | solution.py:297
  817.6 110.8 %collective-permute-start.20 = (f32[32,64,128]{2,1,0:T(8,128)}, f32[32,64,128]{2,1,0:T(8,128)}, u32[]{:S(2)}, u32[]{:S(2)}) collective-permute-start(f32[32,64,128]{2,1,0:T(8,128)} %get-tuple-element.98), channel_id=1, source_target_pairs={{0,1},{1,2},{2,3},{3,0},{4,5},{5,6},{6,7},{7,4},{8,9},{9,10},{10,1... | collective-permute-start | bytes 3145736 | tf_op jit(solution)/shard_map/ppermute | solution.py:297
  817.6 145.2 %collective-permute-start.23 = (f32[32,64,128]{2,1,0:T(8,128)}, f32[32,64,128]{2,1,0:T(8,128)}, u32[]{:S(2)}, u32[]{:S(2)}) collective-permute-start(f32[32,64,128]{2,1,0:T(8,128)} %get-tuple-element.101), channel_id=1, source_target_pairs={{0,2},{1,3},{2,0},{3,1},{4,6},{5,7},{6,4},{7,5},{8,10},{9,11},{10,... | collective-permute-start | bytes 3145736 | tf_op jit(solution)/shard_map/ppermute | solution.py:297
  817.9 144.9 %collective-permute-start.26 = (f32[32,64,128]{2,1,0:T(8,128)}, f32[32,64,128]{2,1,0:T(8,128)}, u32[]{:S(2)}, u32[]{:S(2)}) collective-permute-start(f32[32,64,128]{2,1,0:T(8,128)} %get-tuple-element.104), channel_id=1, source_target_pairs={{0,3},{1,0},{2,1},{3,2},{4,7},{5,4},{6,5},{7,6},{8,11},{9,8},{10,9... | collective-permute-start | bytes 3145736 | tf_op jit(solution)/shard_map/ppermute | solution.py:297
  861.7 183.7 %collective-permute-start.30 = (f32[32,8,128]{2,1,0:T(8,128)}, f32[32,8,128]{2,1,0:T(8,128)S(1)}, u32[]{:S(2)}, u32[]{:S(2)}) collective-permute-start(f32[32,8,128]{2,1,0:T(8,128)} %get-tuple-element.110), channel_id=1, source_target_pairs={{0,1},{1,2},{2,3},{3,0},{4,5},{5,6},{6,7},{7,4},{8,9},{9,10},{10,1... | collective-permute-start | bytes 393224 | tf_op jit(solution)/shard_map/ppermute | solution.py:297
  884.4 161.0 %collective-permute-start.31 = (f32[32,8,128]{2,1,0:T(8,128)}, f32[32,8,128]{2,1,0:T(8,128)}, u32[]{:S(2)}, u32[]{:S(2)}) collective-permute-start(f32[32,8,128]{2,1,0:T(8,128)} %get-tuple-element.111), channel_id=1, source_target_pairs={{0,2},{1,3},{2,0},{3,1},{4,6},{5,7},{6,4},{7,5},{8,10},{9,11},{10,... | collective-permute-start | bytes 393224 | tf_op jit(solution)/shard_map/ppermute | solution.py:297
  928.4 64.8 %collective-permute-start.39 = (f32[32,16,128]{2,1,0:T(8,128)}, f32[32,16,128]{2,1,0:T(8,128)S(1)}, u32[]{:S(2)}, u32[]{:S(2)}) collective-permute-start(f32[32,16,128]{2,1,0:T(8,128)} %get-tuple-element.122), channel_id=1, source_target_pairs={{0,1},{1,2},{2,3},{3,0},{4,5},{5,6},{6,7},{7,4},{8,9},{9,10},{10,1... | collective-permute-start | bytes 786440 | tf_op jit(solution)/shard_map/ppermute | solution.py:297
  (79 other events, 2163.7 us)
